TPU v7x, 32 devices: a whole 2x2x4 slice. The times are simulated.
32 devices in a mesh: groups: 2 (over y), users: 4 (over z), routers: 2 (over x), heads: 2 (over core).
Axes of the slice: x: 2, y: 2, z: 4, core: 2. Of those that a mesh axis runs over, the one named last changes fastest.
Arguments:
- items: bfloat16 [64, 64, 1024], P(('groups', 'users', 'routers')), parts along dimension 0, may hold values from -6 to 6
- block_owner: int32 [64, 1], P(('groups', 'users', 'routers')), parts along dimension 0, may hold values from 0 to 3; in each aligned block of 4 rows (0 to 3, 4 to 7, ...) at most 2 rows name the same one
- block_user: int32 [64], P(('groups', 'users', 'routers')), parts along dimension 0, may hold values from 0 to 1
- block_fill: int32 [64], P(('groups', 'users', 'routers')), parts along dimension 0, may hold values from 1 to 64
- prefix_keys: bfloat16 [16, 256, 1024], P(('groups', 'users'), None, 'heads'), parts along dimension 0, may hold values from -6 to 6
- prefix_values: bfloat16 [16, 256, 1024], P(('groups', 'users'), None, 'heads'), parts along dimension 0, may hold values from -6 to 6
- w_in: bfloat16 [4, 1024, 1024], P(None, 'routers', 'heads'), may hold values from -0.1875 to 0.1875
- attn_gain: bfloat16 [1024], P('heads'), may hold values from 0.25 to 1.75
- w_o: bfloat16 [1024, 1024], P('heads', 'routers'), may hold values from -0.1875 to 0.1875
- mlp_gain: bfloat16 [1024], replicated, may hold values from 0.25 to 1.75
- w_one: bfloat16 [1024, 256], replicated, may hold values from -0.1875 to 0.1875
- w_two: bfloat16 [256], replicated, may hold values from -0.375 to 0.375
Outputs:
- scores: float32 [64, 64], P(('groups', 'users', 'routers')), parts along dimension 0
There are 2 independent parts, one for each index of `groups`. A program takes and returns all parts, laid end to end along the dimension named above; an argument that names none is the same for every part. Nothing has to cross between parts.
Inputs may be any that keep to these rules, and one draw needn't show every extreme that they name: `block_owner`: within the rows of one device (aligned blocks of 4 blocks), no owner is named by more than 2 rows, and in every draw some owner is named by exactly 2 rows of some device.
All inputs are finite; a program needn't handle non-finite values.
Results may differ from a plain program's by a relative error of at most 0.005.
Values may be sent and summed in bfloat16 or wider, within the bound.
A program may use at most 64 MiB of HBM per device.

v0:
```python
import jax
import jax.numpy as jnp
from jax import lax
from jax.sharding import PartitionSpec as P

D = 1024
HEAD_DIM = 128
CAP = 2
HD = 1024


EPSILON = 1e-05


def prefix_attention(group_queries, group_users, prefix_keys, prefix_values):
    group_size, block_width, half_width = group_queries.shape
    heads_here = half_width // HEAD_DIM
    safe_user = jnp.maximum(group_users, 0)
    user_keys = jnp.take(prefix_keys, safe_user, axis=0)
    user_values = jnp.take(prefix_values, safe_user, axis=0)
    query_heads = group_queries.reshape(group_size, block_width, heads_here, HEAD_DIM)
    key_heads = user_keys.reshape(group_size, -1, heads_here, HEAD_DIM)
    value_heads = user_values.reshape(group_size, -1, heads_here, HEAD_DIM)
    raw_scores = jnp.einsum(
        "gqhd,gkhd->ghqk", query_heads, key_heads, preferred_element_type=jnp.float32
    ) * HEAD_DIM ** (-0.5)
    weights = jax.nn.silu(raw_scores).astype(jnp.bfloat16)
    summed = jnp.einsum("ghqk,gkhd->gqhd", weights, value_heads, preferred_element_type=jnp.float32)
    return summed.reshape(group_size, block_width, half_width).astype(jnp.bfloat16)


def local(
    items,
    block_owner,
    block_user,
    block_fill,
    prefix_keys,
    prefix_values,
    w_in,
    attn_gain,
    w_o,
    mlp_gain,
    w_one,
    w_two,
):
    blocks, block_width, model_width = items.shape
    row_count = blocks * block_width
    half_width = w_in.shape[2]
    heads_here = half_width // HEAD_DIM
    peer_count = lax.axis_size("users")
    slot_count = peer_count * CAP
    score_scale = HEAD_DIM ** (-0.5)
    flat_items = items.reshape(row_count, model_width)
    projected = jnp.einsum(
        "rk,pkc->prc",
        flat_items,
        lax.all_gather(w_in, "routers", axis=1, tiled=True),
        preferred_element_type=jnp.float32,
    )
    activated = jax.nn.silu(projected)
    queries = activated[0].astype(jnp.bfloat16)
    target = block_owner[:, 0]
    earlier = lax.broadcasted_iota(jnp.int32, (blocks, blocks), 1) < lax.broadcasted_iota(
        jnp.int32, (blocks, blocks), 0
    )
    same_target = target[:, None] == target[None, :]
    dest_rank = jnp.sum((same_target & earlier).astype(jnp.int32), axis=1)
    position = target * CAP + dest_rank
    selector = lax.broadcasted_iota(jnp.int32, (slot_count, blocks), 0) == position[None, :]
    block_queries = queries.reshape(blocks, block_width * half_width)
    outgoing = jnp.dot(
        selector.astype(jnp.bfloat16), block_queries, preferred_element_type=jnp.float32
    ).astype(jnp.bfloat16)
    outgoing = outgoing.reshape(peer_count, CAP, block_width, half_width)
    slot_user = jnp.sum(jnp.where(selector, block_user[None, :] + 1, 0), axis=1) - 1
    slot_user = slot_user.reshape(peer_count, CAP)
    arrived = lax.all_to_all(outgoing, "users", split_axis=0, concat_axis=0, tiled=True)
    arrived_users = lax.all_to_all(slot_user, "users", split_axis=0, concat_axis=0, tiled=True)
    sources, per_source = arrived_users.shape
    total_slots = sources * per_source
    flat_queries = arrived.reshape(total_slots, block_width, half_width)
    flat_users = arrived_users.reshape(total_slots)
    packing = jnp.argsort((flat_users < 0).astype(jnp.int32), stable=True)
    used_slots = jnp.sum((flat_users >= 0).astype(jnp.int32))
    packed_queries = jnp.take(flat_queries, packing, axis=0)
    packed_users = jnp.take(flat_users, packing, axis=0)
    needed = (used_slots + 3) // 4

    def attend_group(group_index, buffer):
        first_slot = group_index * 4
        group_queries = lax.dynamic_slice_in_dim(packed_queries, first_slot, 4, 0)
        group_users = lax.dynamic_slice_in_dim(packed_users, first_slot, 4, 0)
        result = prefix_attention(group_queries, group_users, prefix_keys, prefix_values)
        return lax.dynamic_update_slice_in_dim(buffer, result, first_slot, 0)

    packed_out = lax.fori_loop(
        0, needed, attend_group, jnp.zeros((total_slots, block_width, half_width), jnp.bfloat16)
    )
    inverse = jnp.argsort(packing)
    attended_slots = jnp.take(packed_out, inverse, axis=0)
    returned = lax.all_to_all(
        attended_slots.reshape(sources, per_source, block_width, half_width),
        "users",
        split_axis=0,
        concat_axis=0,
        tiled=True,
    )
    prefix_part = jnp.take(returned.reshape(slot_count, block_width * half_width), position, axis=0)
    prefix_part = prefix_part.reshape(row_count, heads_here, HEAD_DIM).astype(jnp.float32)
    query_heads = queries.astype(jnp.float32).reshape(row_count, heads_here, HEAD_DIM)
    self_keys = activated[1].reshape(row_count, heads_here, HEAD_DIM)
    self_values = activated[2].reshape(row_count, heads_here, HEAD_DIM)
    own_term = (
        jax.nn.silu(jnp.sum(query_heads * self_keys, axis=-1) * score_scale)[..., None]
        * self_values
    )
    attended = (prefix_part + own_term).reshape(row_count, half_width)
    totals = lax.psum((jnp.sum(attended, axis=1), jnp.sum(attended * attended, axis=1)), "heads")
    row_mean = totals[0] / HD
    row_var = totals[1] / HD - row_mean * row_mean
    gated = (
        (attended - row_mean[:, None])
        * lax.rsqrt(row_var + EPSILON)[:, None]
        * attn_gain.astype(jnp.float32)
        * activated[3]
    ).astype(jnp.bfloat16)
    partial_out = jnp.dot(
        gated,
        lax.all_gather(w_o, "routers", axis=1, tiled=True),
        preferred_element_type=jnp.float32,
    )
    mixed = lax.psum(partial_out, "heads")
    residual = flat_items.astype(jnp.float32) + mixed
    row_scale = lax.rsqrt(jnp.sum(residual * residual, axis=1) / D + EPSILON)
    normed = (residual * row_scale[:, None] * mlp_gain.astype(jnp.float32)).astype(jnp.bfloat16)
    hidden = jax.nn.silu(jnp.dot(normed, w_one, preferred_element_type=jnp.float32)).astype(
        jnp.bfloat16
    )
    block_scores = jnp.dot(hidden, w_two, preferred_element_type=jnp.float32).reshape(
        blocks, block_width
    )
    is_valid = lax.broadcasted_iota(jnp.int32, (blocks, block_width), 1) < block_fill[:, None]
    return jnp.where(is_valid, block_scores, jnp.zeros_like(block_scores))


def solution(mesh):
    placed = (
        P(("groups", "users", "routers"), None, None),
        P(("groups", "users", "routers"), None),
        P(("groups", "users", "routers")),
        P(("groups", "users", "routers")),
        P(("groups", "users"), None, "heads"),
        P(("groups", "users"), None, "heads"),
        P(None, "routers", "heads"),
        P("heads"),
        P("heads", "routers"),
        P(),
        P(),
        P(),
    )
    return jax.shard_map(
        local,
        mesh=mesh,
        in_specs=placed,
        out_specs=P(("groups", "users", "routers"), None),
        check_vma=False,
    )
```

profile of v0, /device:TPU:0, one launch (start us, length us, event | category | flops | bytes accessed | tf_op | source)
XLA Modules:
  0.0 166.5 jit_solution(10524344665358077682)
XLA Ops:
  6.5 4.2 %copy.36 = bf16[4,512,512]{1,2,0:T(8,128)(2,1)} copy(bf16[4,512,512]{2,1,0:T(8,128)(2,1)} %param.24) | data formatting | bytes 4194304 | tf_op args[6]
  12.4 6.3 %all-to-all-start = ((s32[4,1,2]{2,1,0:T(1,128)}), s32[4,1,2]{2,1,0:T(1,128)S(1)}, u32[]{:S(2)}, u32[]{:S(2)}) async-start(s32[4,1,2]{2,1,0:T(1,128)} %bitcast.5), calls=%async_computation | async-start | bytes 4096 | tf_op jit(solution)/shard_map/all_to_all | solution.py:78
  19.4 4.8 %all-to-all-done = s32[4,1,2]{2,1,0:T(1,128)S(1)} async-done(((s32[4,1,2]{2,1,0:T(1,128)}), s32[4,1,2]{2,1,0:T(1,128)S(1)}, u32[]{:S(2)}, u32[]{:S(2)}) %all-to-all-start) | async-done | bytes 64 | tf_op jit(solution)/shard_map/all_to_all | solution.py:78
  24.7 1.3 fusion.40
  26.1 1.0 sort.34
  27.1 43.4 %all-gather.3.cloned.1.call-done = bf16[4,1024,512]{1,2,0:T(8,128)(2,1)} async-done(((bf16[4,512,512]{1,2,0:T(8,128)(2,1)}), bf16[4,1024,512]{1,2,0:T(8,128)(2,1)}) %all-gather.3.cloned.1.call-update) | async-done | bytes 4194320 | tf_op jit(solution)/shard_map/all_gather | solution.py:57
  70.4 3.6 %bitcast_multiply_fusion = f32[4,256,512]{1,2,0:T(8,128)S(1)} fusion(bf16[4,1024,512]{1,2,0:T(8,128)(2,1)} %all-gather.3.cloned.1.call-done, bf16[256,1024,1]{1,0,2:T(8,128)(2,1)S(1)} %bitcast.106), kind=kOutput, calls=%fused_computation.28 | convolution fusion | flops 1075838976 | bytes 6815744 | tf_op jit(solution)/shard_map/rk,pkc->prc/dot_general | solution.py:54
  74.0 1.3 copy-done.5
  77.0 1.0 copy.43
  78.0 4.7 %all-to-all-start.1 = ((bf16[4,2,64,512]{3,2,1,0:T(8,128)(2,1)}), bf16[4,2,64,512]{3,2,1,0:T(8,128)(2,1)S(1)}, u32[]{:S(2)}, u32[]{:S(2)}) async-start(bf16[4,2,64,512]{3,2,1,0:T(8,128)(2,1)} %bitcast.27), calls=%async_computation.1 | async-start | bytes 1048576 | tf_op jit(solution)/shard_map/all_to_all | solution.py:77
  85.0 12.0 %all-to-all-done.1 = bf16[4,2,64,512]{3,2,1,0:T(8,128)(2,1)S(1)} async-done(((bf16[4,2,64,512]{3,2,1,0:T(8,128)(2,1)}), bf16[4,2,64,512]{3,2,1,0:T(8,128)(2,1)S(1)}, u32[]{:S(2)}, u32[]{:S(2)}) %all-to-all-start.1) | async-done | bytes 524320 | tf_op jit(solution)/shard_map/all_to_all | solution.py:77
  99.4 12.2 %while.10 = (s32[]{:T(128)}, bf16[8,64,512]{2,1,0:T(8,128)(2,1)}, s32[]{:T(128)}, s32[8]{0:T(128)S(1)}, bf16[2,256,512]{2,1,0:T(8,128)(2,1)S(1)}, /*index=5*/bf1...) while((s32[]{:T(128)}, bf16[8,64,512]{2,1,0:T(8,128)(2,1)}, ...), condition=%wide.region_5.8_spmd, body=%wide.region_4.7_spmd.sunk | while | flops 136971280 | bytes 13635875 | solution.py:96
  100.7 1.5 select_bitcast_fusion.3
  102.3 2.5 %fusion.55 = bf16[4,4,8,8,128]{4,3,2,1,0:T(8,128)(2,1)S(1)} fusion(bf16[4,32,4,8,128]{4,3,2,1,0:T(8,128)(2,1)} %get-tuple-element.135, bf16[4,32,4,8,128]{4,3,2,1,0:T(8,128)(2,1)} %get-tuple-element.136, bf16[8,64,512]{2,1,0:T(8,128)(2,1)} %get-tuple-element.164, s32[]{:T(128)S(6)} %select_n.93), kind=kOutput, calls=%fused_computation.8.clone.1 | convolution fusion | flops 135921664 | bytes 2621444 | tf_op jit(solution)/shard_map/while/body/ghqk,gkhd->gqhd/dot_general | solution.py:28
  106.8 1.5 select_bitcast_fusion.3
  108.4 2.5 %fusion.55 = bf16[4,4,8,8,128]{4,3,2,1,0:T(8,128)(2,1)S(1)} fusion(bf16[4,32,4,8,128]{4,3,2,1,0:T(8,128)(2,1)} %get-tuple-element.135, bf16[4,32,4,8,128]{4,3,2,1,0:T(8,128)(2,1)} %get-tuple-element.136, bf16[8,64,512]{2,1,0:T(8,128)(2,1)} %get-tuple-element.164, s32[]{:T(128)S(6)} %select_n.93), kind=kOutput, calls=%fused_computation.8.clone.1 | convolution fusion | flops 135921664 | bytes 2621444 | tf_op jit(solution)/shard_map/while/body/ghqk,gkhd->gqhd/dot_general | solution.py:28
  111.6 1.7 %gather_fusion.5 = bf16[8,64,512]{2,1,0:T(8,128)(2,1)S(1)} fusion(bf16[8,64,512]{2,1,0:T(8,128)(2,1)} %get-tuple-element.174, s32[1024]{0:T(1024)S(1)} %pad_clamp_fusion.2), kind=kCustom, calls=%fused_computation.2.clone | custom fusion | bytes 1048608 | tf_op jit(solution)/shard_map/jit(_take)/gather | solution.py:100
  114.2 3.5 %all-to-all-start.2 = ((bf16[4,2,64,512]{3,2,1,0:T(8,128)(2,1)}), bf16[4,2,64,512]{3,2,1,0:T(8,128)(2,1)S(1)}, u32[]{:S(2)}, u32[]{:S(2)}) async-start(bf16[4,2,64,512]{3,2,1,0:T(8,128)(2,1)} %bitcast.9), calls=%async_computation.2 | async-start | bytes 1048576 | tf_op jit(solution)/shard_map/all_to_all | solution.py:101
  118.0 13.7 %all-to-all-done.2 = bf16[4,2,64,512]{3,2,1,0:T(8,128)(2,1)S(1)} async-done(((bf16[4,2,64,512]{3,2,1,0:T(8,128)(2,1)}), bf16[4,2,64,512]{3,2,1,0:T(8,128)(2,1)S(1)}, u32[]{:S(2)}, u32[]{:S(2)}) %all-to-all-start.2) | async-done | bytes 524320 | tf_op jit(solution)/shard_map/all_to_all | solution.py:101
  133.8 2.5 %all-reduce = (f32[256]{0:T(256)S(1)}, f32[256]{0:T(256)S(1)}) all-reduce(f32[256]{0:T(256)S(1)} %get-tuple-element.51, f32[256]{0:T(256)S(1)} %get-tuple-element.50), channel_id=1, replica_groups=mesh['groups'=2,'users'=4,'routers'=2,'heads'=2] {'heads'}, use_global_device_ids=true, to_apply=%region_11.14 | all-reduce | flops 512 | bytes 4096 | tf_op jit(solution)/shard_map/psum | solution.py:118
  136.3 2.8 %fusion.27 = f32[256,1024]{1,0:T(8,128)} fusion(bf16[512,1024]{1,0:T(8,128)(2,1)} %all-gather.5.cloned.1.call-done, f32[4,256,512]{1,2,0:T(8,128)S(1)} %copy-done.6, f32[256,512]{0,1:T(8,128)S(1)} %get-tuple-element.72, f32[512]{0:T(512)S(1)} %convert_element_type.80, f32[256]{0:T(256)S(1)} %get-tuple-element.82, f32[256]{0:T(256)S(1)} %get-tuple-element.81), kind=kOutput, calls=%fused_computation.50 | convolution fusion | flops 269090816 | bytes 3149824 | tf_op jit(solution)/shard_map/dot_general | solution.py:127
  139.2 16.7 %all-reduce.3.cloned.1.call-done = f32[256,1024]{1,0:T(8,128)} async-done(((f32[256,1024]{1,0:T(8,128)}), f32[256,1024]{1,0:T(8,128)}) %all-reduce.3.cloned.1.call-update) | async-done | bytes 1048592 | tf_op jit(solution)/shard_map/psum | solution.py:132
  155.9 1.6 multiply_reduce_fusion
  157.5 1.7 %fusion.29 = f32[1,256]{1,0:T(1,128)S(1)} fusion(bf16[256,1]{0,1:T(2,128)(2,1)S(1)} %reshape.186, bf16[1024,256]{1,0:T(8,128)(2,1)S(1)} %copy-done, f32[256,1024]{1,0:T(8,128)} %all-reduce.3.cloned.1.call-done, bf16[256,1024]{1,0:T(8,128)(2,1)S(1)} %bitcast.107, f32[1024]{0:T(1024)S(1)} %convert_element_type.82, f32[256]{0:T(256)S(1)} %add_rsqrt_fusion), kind=kOutput, calls=%fused_computation.52 | convolution fusion | flops 135987200 | bytes 2103808 | tf_op jit(solution)/shard_map/dot_general | solution.py:139
  (92 shorter events, 16.7 us)
Async XLA Ops:
  6.5 151.0 %copy-start = (bf16[1024,256]{1,0:T(8,128)(2,1)S(1)}, bf16[1024,256]{1,0:T(8,128)(2,1)}, u32[]{:S(2)}) copy-start(bf16[1024,256]{1,0:T(8,128)(2,1)} %param.28) | copy-start | bytes 1572868
  6.5 63.9 %all-gather.3.cloned.1.call-start = ((), (), s32[]{:S(2)}) async-start(), calls=%async_computation.3 | async-start | bytes 6291456 | tf_op jit(solution)/shard_map/all_gather | solution.py:57
  10.7 0.7 copy-start.10
  10.7 0.8 copy-start.12
  10.8 59.7 %copy-start.7 = (bf16[4,64,1024]{2,1,0:T(8,128)(2,1)S(1)}, bf16[4,64,1024]{2,1,0:T(8,128)(2,1)}, u32[]{:S(2)}) copy-start(bf16[4,64,1024]{2,1,0:T(8,128)(2,1)} %param.18) | copy-start | bytes 1572868
  12.4 11.8 %all-to-all-start = ((s32[4,1,2]{2,1,0:T(1,128)}), s32[4,1,2]{2,1,0:T(1,128)S(1)}, u32[]{:S(2)}, u32[]{:S(2)}) async-start(s32[4,1,2]{2,1,0:T(1,128)} %bitcast.5), calls=%async_computation | async-start | bytes 4096 | tf_op jit(solution)/shard_map/all_to_all | solution.py:78
  18.7 117.5 %all-gather.5.cloned.1.call-start = ((), (), s32[]{:S(2)}) async-start(), calls=%async_computation.4 | async-start | bytes 1572864 | tf_op jit(solution)/shard_map/all_gather | solution.py:129
  74.0 1.4 copy-start.5
  78.0 21.4 %copy-start.1 = (bf16[2,256,512]{2,1,0:T(8,128)(2,1)S(1)}, bf16[2,256,512]{2,1,0:T(8,128)(2,1)}, u32[]{:S(2)}) copy-start(bf16[2,256,512]{2,1,0:T(8,128)(2,1)} %param.23) | copy-start | bytes 1572868
  78.0 21.4 %copy-start.2 = (bf16[2,256,512]{2,1,0:T(8,128)(2,1)S(1)}, bf16[2,256,512]{2,1,0:T(8,128)(2,1)}, u32[]{:S(2)}) copy-start(bf16[2,256,512]{2,1,0:T(8,128)(2,1)} %param.22) | copy-start | bytes 1572868
  78.0 19.1 %all-to-all-start.1 = ((bf16[4,2,64,512]{3,2,1,0:T(8,128)(2,1)}), bf16[4,2,64,512]{3,2,1,0:T(8,128)(2,1)S(1)}, u32[]{:S(2)}, u32[]{:S(2)}) async-start(bf16[4,2,64,512]{3,2,1,0:T(8,128)(2,1)} %bitcast.27), calls=%async_computation.1 | async-start | bytes 1048576 | tf_op jit(solution)/shard_map/all_to_all | solution.py:77
  102.3 3.2 %copy-start.3 = (bf16[2,256,512]{2,1,0:T(8,128)(2,1)S(1)}, bf16[2,256,512]{2,1,0:T(8,128)(2,1)}, u32[]{:S(2)}) copy-start(bf16[2,256,512]{2,1,0:T(8,128)(2,1)} %get-tuple-element.184) | copy-start | bytes 1572868 | tf_op jit(solution)/shard_map/while
  108.4 3.2 %copy-start.3 = (bf16[2,256,512]{2,1,0:T(8,128)(2,1)S(1)}, bf16[2,256,512]{2,1,0:T(8,128)(2,1)}, u32[]{:S(2)}) copy-start(bf16[2,256,512]{2,1,0:T(8,128)(2,1)} %get-tuple-element.184) | copy-start | bytes 1572868 | tf_op jit(solution)/shard_map/while
  111.6 6.3 %copy-start.11 = (bf16[512]{0:T(512)(128)(2,1)S(1)}, bf16[512]{0:T(512)(128)(2,1)}, u32[]{:S(2)}) copy-start(bf16[512]{0:T(512)(128)(2,1)} %param.25) | copy-start | bytes 3076
  111.6 6.3 %copy-start.4 = (f32[1,256,512]{1,2,0:T(8,128)S(1)}, f32[1,256,512]{1,2,0:T(8,128)}, u32[]{:S(2)}) copy-start(f32[1,256,512]{1,2,0:T(8,128)} %get-tuple-element.77) | copy-start | bytes 1572868
  114.2 17.5 %all-to-all-start.2 = ((bf16[4,2,64,512]{3,2,1,0:T(8,128)(2,1)}), bf16[4,2,64,512]{3,2,1,0:T(8,128)(2,1)S(1)}, u32[]{:S(2)}, u32[]{:S(2)}) async-start(bf16[4,2,64,512]{3,2,1,0:T(8,128)(2,1)} %bitcast.9), calls=%async_computation.2 | async-start | bytes 1048576 | tf_op jit(solution)/shard_map/all_to_all | solution.py:101
  117.7 38.2 %all-reduce.3.cloned.1.call-start = ((), (), s32[]{:S(2)}) async-start(), calls=%async_computation.5 | async-start | bytes 2097152 | tf_op jit(solution)/shard_map/psum | solution.py:132
  132.0 1.6 copy-start.6
  136.3 2.8 %copy-start.9 = (bf16[1024]{0:T(1024)(128)(2,1)S(1)}, bf16[1024]{0:T(1024)(128)(2,1)}, u32[]{:S(2)}) copy-start(bf16[1024]{0:T(1024)(128)(2,1)} %param.27) | copy-start | bytes 6148
  136.3 2.9 %copy-start.14 = (bf16[256]{0:T(256)(128)(2,1)S(1)}, bf16[256]{0:T(256)(128)(2,1)}, u32[]{:S(2)}) copy-start(bf16[256]{0:T(256)(128)(2,1)} %param.29) | copy-start | bytes 1540
  139.1 18.4 %copy-start.8 = (bf16[4,64,1024]{2,1,0:T(8,128)(2,1)S(1)}, bf16[4,64,1024]{2,1,0:T(8,128)(2,1)}, u32[]{:S(2)}) copy-start(bf16[4,64,1024]{2,1,0:T(8,128)(2,1)} %param.18) | copy-start | bytes 1572868
  139.1 20.2 %copy-start.13 = (s32[4]{0:T(128)S(1)}, s32[4]{0:T(128)}, u32[]{:S(2)}) copy-start(s32[4]{0:T(128)} %param.21) | copy-start | bytes 52
Sparse Core Ops, SparseCore 0:
  10.9 59.4 all-gather.2
  72.0 21.2 all-gather.4
  139.2 16.6 all-reduce.2
where the time goes:
time: 167 us
  waiting for transfers between devices  91.3 us (55%)
  local copies, waits for them, and re-layouts  18.6 us (11%)
  starting transfers between devices  14.6 us (9%)
  between operations  14 us (8%)
  matrix products  13.5 us (8%)
  other arithmetic  12 us (7%)
  blocking collectives  2.46 us (1%)
    all_gather x1, waiting for transfers between devices, local(): lax.all_gather(w_in, 'routers', axis=1, tiled=True)  43.4 us
    psum x1, waiting for transfers between devices, local(): mixed = lax.psum(partial_out, 'heads')  16.7 us
    all_to_all x1, waiting for transfers between devices, local(): lax.all_to_all(attended_slots.reshape(sources, per_source, block_width, h...  13.7 us
    all_to_all x1, waiting for transfers between devices, local(): lax.all_to_all(outgoing, 'users', split_axis=0, concat_axis=0, tiled=True)  12 us
    unnamed x32, local copies, waits for them, and re-layouts  7.95 us
    all_to_all x1, starting transfers between devices, local(): lax.all_to_all(slot_user, 'users', split_axis=0, concat_axis=0, tiled=True)  6.35 us
    dot_general x2, matrix products, prefix_attention(): jnp.einsum('ghqk,gkhd->gqhd', weights, value_heads, preferred_element_typ...  4.92 us
    all_to_all x1, waiting for transfers between devices, local(): lax.all_to_all(slot_user, 'users', split_axis=0, concat_axis=0, tiled=True)  4.76 us
  transfers between devices with their start and end apart: 6, of which 5 were waited for; matrix products, arithmetic and copies ran while one was open for 18% of the time, Pallas kernels for 0%

commit v1 on v0

v1 whole, which is shorter than its diff:
```python
import functools

import jax
import jax.numpy as jnp
from jax import lax
from jax.experimental import pallas as pl
from jax.experimental.pallas import tpu as pltpu
from jax.sharding import PartitionSpec as P

HEAD_DIM = 128
CAP = 2
EPSILON = 1e-05
SUB = 2
F32 = jnp.float32
BF16 = jnp.bfloat16
MESH = pl.DeviceIdType.MESH


def silu(v):
    return 0.5 * v * (1.0 + jnp.tanh(0.5 * v))


def scorer(
    sizes,
    items_ref,
    owner_ref,
    user_ref,
    fill_ref,
    keys_ref,
    values_ref,
    w_in_ref,
    attn_gain_ref,
    w_o_ref,
    mlp_gain_ref,
    w_one_ref,
    w_two_ref,
    out_ref,
    items_v,
    out_slots,
    x_all,
    mask_out,
    mask_all,
    keys_v,
    values_v,
    w_all,
    wo_all,
    w_one_v,
    q_v,
    sk_v,
    sv_v,
    gates_v,
    att_v,
    gated_v,
    stat_out,
    stat_in,
    part_out,
    part_own,
    part_in,
    sc_out,
    ret,
    local_sem,
    z_send,
    z_recv,
    m_send,
    m_recv,
    rel_send,
    rel_recv,
    x_send,
    x_recv,
    y_send,
    y_recv,
    st_sem,
    po_send,
    po_recv,
    sc_send,
    sc_recv,
):
    groups, users, routers, heads = sizes
    g = lax.axis_index("groups")
    me = lax.axis_index("users")
    r = lax.axis_index("routers")
    h = lax.axis_index("heads")
    mate = 1 - h
    blocks, width, model = items_v.shape
    slots = x_all.shape[0]
    half_width = q_v.shape[1]
    heads_here = half_width // HEAD_DIM
    hd_all = half_width * heads
    rows = slots * width
    depth = w_all.shape[2]
    out_cols = wo_all.shape[2]
    wh = width // heads
    scale = HEAD_DIM ** (-0.5)
    positions = keys_v.shape[0] * keys_v.shape[1]
    per_user = keys_v.shape[1]

    c_items = pltpu.make_async_copy(items_ref, items_v, local_sem.at[0])
    c_items.start()

    barrier = pltpu.get_barrier_semaphore()
    count = 0
    for j in range(1, routers):
        pl.semaphore_signal(
            barrier, inc=1, device_id={"routers": lax.rem(r + j, routers)}, device_id_type=MESH
        )
        count += 1
    for i in range(1, groups):
        pl.semaphore_signal(
            barrier, inc=1, device_id={"groups": lax.rem(g + i, groups)}, device_id_type=MESH
        )
        count += 1
    pl.semaphore_signal(barrier, inc=1, device_id={"heads": mate}, device_id_type=MESH)
    count += 1
    for k in range(1, users):
        for e in range(heads):
            pl.semaphore_signal(
                barrier,
                inc=1,
                device_id={"users": lax.rem(me + k, users), "heads": e},
                device_id_type=MESH,
            )
            count += 1
    c_keys = pltpu.make_async_copy(keys_ref, keys_v, local_sem.at[1])
    c_values = pltpu.make_async_copy(values_ref, values_v, local_sem.at[2])
    c_win = pltpu.make_async_copy(w_in_ref, w_all.at[:, r], local_sem.at[3])
    c_wo = pltpu.make_async_copy(w_o_ref, wo_all.at[r], local_sem.at[4])
    c_one = pltpu.make_async_copy(w_one_ref, w_one_v, local_sem.at[5])
    pl.semaphore_wait(barrier, count)

    pieces = [(p, s) for p in range(5) for s in range(SUB)]

    def in_rows(owner_group, s):
        share = depth // groups // SUB
        return pl.ds(pl.multiple_of((owner_group * SUB + s) * share, share), share)

    def out_rows(owner_group, s):
        share = half_width // groups // SUB
        return pl.ds(pl.multiple_of((owner_group * SUB + s) * share, share), share)

    def weight_slot(owner_router, owner_group, p, s):
        if p < 4:
            return w_all.at[p, owner_router, in_rows(owner_group, s), :]
        return wo_all.at[owner_router, out_rows(owner_group, s), :]

    def x_copy(j, t, source_router):
        p, s = pieces[t]
        if p < 4:
            src = w_in_ref.at[p, in_rows(g, s), :]
        else:
            src = w_o_ref.at[out_rows(g, s), :]
        return pltpu.make_async_remote_copy(
            src_ref=src,
            dst_ref=weight_slot(source_router, g, p, s),
            send_sem=x_send.at[j, t],
            recv_sem=x_recv.at[j, t],
            device_id={"routers": lax.rem(r + j, routers)},
            device_id_type=MESH,
        )

    def y_copy(i, j, t, owner_group):
        p, s = pieces[t]
        spot = weight_slot(lax.rem(r - j + routers, routers), owner_group, p, s)
        return pltpu.make_async_remote_copy(
            src_ref=spot,
            dst_ref=spot,
            send_sem=y_send.at[i, j, t],
            recv_sem=y_recv.at[i, j, t],
            device_id={"groups": lax.rem(g + i, groups)},
            device_id_type=MESH,
        )

    for t in range(len(pieces)):
        for j in range(1, routers):
            x_copy(j, t, r).start()
    for c in (c_win, c_keys, c_values, c_wo, c_one):
        c.start()

    owners = [owner_ref[b, 0] for b in range(blocks)]
    ranks = []
    for b in range(blocks):
        rank = jnp.int32(0)
        for a in range(b):
            rank = rank + jnp.where(owners[a] == owners[b], 1, 0)
        ranks.append(rank)

    def slot_source(dest, cap):
        index, user = jnp.int32(0), jnp.int32(-1)
        for b in range(blocks):
            hit = (owners[b] == dest) & (ranks[b] == cap)
            index = jnp.where(hit, b, index)
            user = jnp.where(hit, user_ref[b], user)
        return index, user

    lane_user = lax.broadcasted_iota(jnp.int32, (1, positions), 1) // per_user
    mask_copies, item_copies = {}, {}

    def z_copy(k, source):
        return pltpu.make_async_remote_copy(
            src_ref=out_slots.at[k],
            dst_ref=x_all.at[pl.ds(source * CAP, CAP), pl.ds(pl.multiple_of(h * wh, wh), wh), :],
            send_sem=z_send.at[k],
            recv_sem=z_recv.at[k],
            device_id={"users": lax.rem(me + k, users)},
            device_id_type=MESH,
        )

    def m_copy(k, source):
        return pltpu.make_async_remote_copy(
            src_ref=mask_out.at[k],
            dst_ref=mask_all.at[source],
            send_sem=m_send.at[k],
            recv_sem=m_recv.at[k],
            device_id={"users": lax.rem(me + k, users)},
            device_id_type=MESH,
        )

    def relay_copy(k, part):
        source = lax.rem(me - k + users, users)
        spot = x_all.at[pl.ds(source * CAP, CAP), pl.ds(pl.multiple_of(part * wh, wh), wh), :]
        return pltpu.make_async_remote_copy(
            src_ref=spot,
            dst_ref=spot,
            send_sem=rel_send.at[k],
            recv_sem=rel_recv.at[k],
            device_id={"heads": mate},
            device_id_type=MESH,
        )

    c_items.wait()
    for k in list(range(1, users)) + [0]:
        dest = lax.rem(me + k, users)
        for cap in range(CAP):
            index, user = slot_source(dest, cap)
            line = jnp.where(lane_user == user, 1.0, 0.0).astype(F32)
            if k == 0:
                x_all[me * CAP + cap] = items_v[index]
                mask_all[me, cap : cap + 1, :] = line
            else:
                out_slots[k, cap] = items_v[index, pl.ds(pl.multiple_of(h * wh, wh), wh), :]
                mask_out[k, cap : cap + 1, :] = line
        if k:
            z_copy(k, me).start()
            m_copy(k, me).start()

    def forward(t):
        for j in range(1, routers):
            x_copy(j, t, lax.rem(r - j + routers, routers)).wait_recv()
            for i in range(1, groups):
                y_copy(i, j, t, g).start()

    def landed(t):
        for j in range(1, routers):
            for i in range(1, groups):
                y_copy(i, j, t, lax.rem(g - i + groups, groups)).wait_recv()

    forward(0)
    forward(1)
    for k in range(1, users):
        z_copy(k, lax.rem(me - k + users, users)).wait_recv()
        relay_copy(k, h).start()
    forward(2)
    for k in range(1, users):
        m_copy(k, lax.rem(me - k + users, users)).wait_recv()
        relay_copy(k, mate).wait_recv()
    c_win.wait()

    tile = 4 * width
    tile_slots = 4
    tiles = rows // tile

    def x_tile(i):
        return x_all[pl.ds(i * tile_slots, tile_slots)].reshape(tile, model)

    def project(p, target):
        @pl.loop(0, tiles)
        def _(i):
            x = x_tile(i)
            total = jnp.zeros((tile, half_width), F32)
            for a in range(routers):
                total = total + jnp.dot(
                    x[:, a * depth : (a + 1) * depth],
                    w_all[p, a],
                    preferred_element_type=F32,
                )
            target[pl.ds(pl.multiple_of(i * tile, tile), tile), :] = silu(total).astype(target.dtype)

    landed(0)
    landed(1)
    project(0, q_v)
    forward(3)
    c_keys.wait()
    c_values.wait()

    @pl.loop(0, tiles)
    def _(i):
        span = pl.ds(pl.multiple_of(i * tile, tile), tile)
        for e in range(heads_here):
            cols = slice(e * HEAD_DIM, (e + 1) * HEAD_DIM)
            raw = lax.dot_general(
                q_v[span, cols],
                keys_v[:, :, cols].reshape(positions, HEAD_DIM),
                (((1,), (1,)), ((), ())),
                preferred_element_type=F32,
            )
            weights = silu(raw * scale)
            parts = []
            for s in range(tile_slots):
                line = mask_all[i * (tile_slots // CAP) + s // CAP, s % CAP : s % CAP + 1, :]
                parts.append(weights[s * width : (s + 1) * width] * line)
            weights = jnp.concatenate(parts, axis=0).astype(BF16)
            att_v[span, cols] = (
                jnp.dot(
                    weights,
                    values_v[:, :, cols].reshape(positions, HEAD_DIM),
                    preferred_element_type=F32,
                )
                .astype(BF16)
                .astype(F32)
            )

    forward(4)
    landed(2)
    landed(3)
    project(1, sk_v)
    forward(5)
    forward(6)
    landed(4)
    landed(5)
    project(2, sv_v)
    forward(7)

    lane = lax.broadcasted_iota(jnp.int32, (tile, 128), 1)

    @pl.loop(0, tiles)
    def _(i):
        span = pl.ds(pl.multiple_of(i * tile, tile), tile)
        total = jnp.zeros((tile, 1), F32)
        square = jnp.zeros((tile, 1), F32)
        for e in range(heads_here):
            cols = slice(e * HEAD_DIM, (e + 1) * HEAD_DIM)
            own = jnp.sum(q_v[span, cols].astype(F32) * sk_v[span, cols], axis=1, keepdims=True)
            att = att_v[span, cols] + silu(own * scale) * sv_v[span, cols]
            att_v[span, cols] = att
            total = total + jnp.sum(att, axis=1, keepdims=True)
            square = square + jnp.sum(att * att, axis=1, keepdims=True)
        stat_out[span, :] = jnp.where(lane == 0, total, square)

    stat_copy = pltpu.make_async_remote_copy(
        src_ref=stat_out,
        dst_ref=stat_in,
        send_sem=st_sem.at[0],
        recv_sem=st_sem.at[1],
        device_id={"heads": mate},
        device_id_type=MESH,
    )
    stat_copy.start()
    forward(8)
    landed(6)
    landed(7)
    project(3, gates_v)
    forward(9)
    stat_copy.wait_recv()

    @pl.loop(0, tiles)
    def _(i):
        span = pl.ds(pl.multiple_of(i * tile, tile), tile)
        both = stat_out[span, :] + stat_in[span, :]
        mean = both[:, 0:1] / hd_all
        var = both[:, 1:2] / hd_all - mean * mean
        gated_v[span, :] = (
            (att_v[span, :] - mean)
            * lax.rsqrt(var + EPSILON)
            * attn_gain_ref[...].astype(F32)
            * gates_v[span, :]
        ).astype(BF16)

    half = rows // heads
    half_tiles = half // tile
    c_wo.wait()

    def part_copy(j):
        return pltpu.make_async_remote_copy(
            src_ref=part_out.at[j],
            dst_ref=part_in.at[j],
            send_sem=po_send.at[j],
            recv_sem=po_recv.at[j],
            device_id={"heads": mate},
            device_id_type=MESH,
        )

    def out_project(j, row_half, target):
        a = lax.rem(r - j + routers, routers)

        @pl.loop(0, half_tiles)
        def _(i):
            src = pl.ds(pl.multiple_of(row_half * half + i * tile, tile), tile)
            target[j, pl.ds(pl.multiple_of(i * tile, tile), tile), :] = jnp.dot(
                gated_v[src, :], wo_all[a], preferred_element_type=F32
            )

    out_project(0, mate, part_out)
    part_copy(0).start()
    out_project(0, h, part_own)
    landed(8)
    landed(9)
    for j in range(1, routers):
        out_project(j, mate, part_out)
        part_copy(j).start()
    for j in range(1, routers):
        out_project(j, h, part_own)
    c_one.wait()
    for j in range(routers):
        part_copy(j).wait_recv()

    sources_tile = tile_slots // CAP
    two = jnp.broadcast_to(w_two_ref[...], (8, w_two_ref.shape[1]))

    @pl.loop(0, half_tiles)
    def _(i):
        span = pl.ds(pl.multiple_of(i * tile, tile), tile)
        x = x_tile(h * half_tiles + i).astype(F32)
        mixed = []
        for a in range(routers):
            j = lax.rem(r - a + routers, routers)
            mixed.append(part_own[j, span, :] + part_in[j, span, :])
        residual = x + jnp.concatenate(mixed, axis=1)
        norm = lax.rsqrt(jnp.sum(residual * residual, axis=1, keepdims=True) / model + EPSILON)
        normed = (residual * norm * mlp_gain_ref[...].astype(F32)).astype(BF16)
        hidden = silu(jnp.dot(normed, w_one_v[...], preferred_element_type=F32)).astype(BF16)
        found = lax.dot_general(two, hidden, (((1,), (1,)), ((), ())), preferred_element_type=F32)
        for s in range(sources_tile):
            sc_out[i * sources_tile + s] = found[:, s * CAP * width : (s + 1) * CAP * width]

    mine = users // heads

    def score_copy(i, e, owner, sem):
        return pltpu.make_async_remote_copy(
            src_ref=sc_out.at[i],
            dst_ref=ret.at[owner],
            send_sem=sc_send.at[i, e],
            recv_sem=sc_recv.at[sem],
            device_id={"users": h * mine + i, "heads": e},
            device_id_type=MESH,
        )

    for i in range(mine):
        target = h * mine + i
        for e in range(heads):
            itself = (target == me) & (h == e)

            @pl.when(jnp.logical_not(itself))
            def _():
                score_copy(i, e, me, me).start()

            @pl.when(itself)
            def _():
                ret[me] = sc_out[i]

    handler = me // mine
    for d in range(users):

        @pl.when(jnp.logical_not((d == me) & (h == handler)))
        def _():
            score_copy(0, 0, d, d).wait_recv()

    position = lax.broadcasted_iota(jnp.int32, (1, width), 1)
    for b in range(blocks):
        tile_in = ret[owners[b]]
        line = tile_in[0:1, 0:width]
        for cap in range(1, CAP):
            line = jnp.where(ranks[b] == cap, tile_in[0:1, cap * width : (cap + 1) * width], line)
        out_ref[b : b + 1, :] = jnp.where(position < fill_ref[b], line, 0.0)

    for t in range(len(pieces)):
        for j in range(1, routers):
            x_copy(j, t, r).wait_send()
            for i in range(1, groups):
                y_copy(i, j, t, g).wait_send()
    for k in range(1, users):
        z_copy(k, me).wait_send()
        m_copy(k, me).wait_send()
        relay_copy(k, h).wait_send()
    stat_copy.wait_send()
    for j in range(routers):
        part_copy(j).wait_send()
    for i in range(mine):
        for e in range(heads):

            @pl.when(jnp.logical_not((h * mine + i == me) & (h == e)))
            def _():
                score_copy(i, e, me, me).wait_send()


def local(
    sizes,
    items,
    block_owner,
    block_user,
    block_fill,
    prefix_keys,
    prefix_values,
    w_in,
    attn_gain,
    w_o,
    mlp_gain,
    w_one,
    w_two,
):
    groups, users, routers, heads = sizes
    blocks, width, model = items.shape
    projections, depth, half_width = w_in.shape
    slots = users * CAP
    rows = slots * width
    half = rows // heads
    out_cols = w_o.shape[1]
    cached, per_user, _ = prefix_keys.shape
    positions = cached * per_user
    pieces = 5 * SUB
    dma = pltpu.SemaphoreType.DMA
    hbm = pl.BlockSpec(memory_space=pl.ANY)
    vmem = pl.BlockSpec(memory_space=pltpu.VMEM)
    smem = pl.BlockSpec(memory_space=pltpu.SMEM)
    scratch = [
        pltpu.VMEM((blocks, width, model), BF16),
        pltpu.VMEM((users, CAP, width // heads, model), BF16),
        pltpu.VMEM((slots, width, model), BF16),
        pltpu.VMEM((users, 8, positions), F32),
        pltpu.VMEM((users, 8, positions), F32),
        pltpu.VMEM(prefix_keys.shape, BF16),
        pltpu.VMEM(prefix_values.shape, BF16),
        pltpu.VMEM((projections, routers, depth, half_width), BF16),
        pltpu.VMEM((routers, half_width, out_cols), BF16),
        pltpu.VMEM(w_one.shape, BF16),
        pltpu.VMEM((rows, half_width), BF16),
        pltpu.VMEM((rows, half_width), F32),
        pltpu.VMEM((rows, half_width), F32),
        pltpu.VMEM((rows, half_width), F32),
        pltpu.VMEM((rows, half_width), F32),
        pltpu.VMEM((rows, half_width), BF16),
        pltpu.VMEM((rows, 128), F32),
        pltpu.VMEM((rows, 128), F32),
        pltpu.VMEM((routers, half, out_cols), F32),
        pltpu.VMEM((routers, half, out_cols), F32),
        pltpu.VMEM((routers, half, out_cols), F32),
        pltpu.VMEM((users // heads, 8, CAP * width), F32),
        pltpu.VMEM((users, 8, CAP * width), F32),
        dma((6,)),
        dma((users,)),
        dma((users,)),
        dma((users,)),
        dma((users,)),
        dma((users,)),
        dma((users,)),
        dma((routers, pieces)),
        dma((routers, pieces)),
        dma((groups, routers, pieces)),
        dma((groups, routers, pieces)),
        dma((2,)),
        dma((routers,)),
        dma((routers,)),
        dma((users // heads, heads)),
        dma((users,)),
    ]
    return pl.pallas_call(
        functools.partial(scorer, sizes),
        out_shape=jax.ShapeDtypeStruct((blocks, width), F32),
        in_specs=[hbm, smem, smem, smem, hbm, hbm, hbm, vmem, hbm, vmem, hbm, vmem],
        out_specs=vmem,
        scratch_shapes=scratch,
        compiler_params=pltpu.CompilerParams(
            collective_id=0, has_side_effects=True, vmem_limit_bytes=62 * 1024 * 1024
        ),
    )(
        items,
        block_owner,
        block_user,
        block_fill,
        prefix_keys,
        prefix_values,
        w_in,
        attn_gain.reshape(1, -1),
        w_o,
        mlp_gain.reshape(1, -1),
        w_one,
        w_two.reshape(1, -1),
    )


def solution(mesh):
    placed = (
        P(("groups", "users", "routers"), None, None),
        P(("groups", "users", "routers"), None),
        P(("groups", "users", "routers")),
        P(("groups", "users", "routers")),
        P(("groups", "users"), None, "heads"),
        P(("groups", "users"), None, "heads"),
        P(None, "routers", "heads"),
        P("heads"),
        P("heads", "routers"),
        P(),
        P(),
        P(),
    )
    sizes = tuple(mesh.shape[name] for name in ("groups", "users", "routers", "heads"))
    return jax.shard_map(
        functools.partial(local, sizes),
        mesh=mesh,
        in_specs=placed,
        out_specs=P(("groups", "users", "routers"), None),
        check_vma=False,
    )
```

time: 167 us -> 59.2 us (0.35)
  waiting for transfers between devices: 91.3 us -> 0 us
  Pallas kernels: 0 us -> 52.6 us
  starting transfers between devices: 14.6 us -> 0 us
  between operations: 14 us -> 0.01 us
  matrix products: 13.5 us -> 0 us
  local copies, waits for them, and re-layouts: 18.6 us -> 6.32 us
  other arithmetic: 12 us -> 0 us
  blocking collectives: 2.46 us -> 0 us
    pallas_call x0 -> x1, Pallas kernels: none -> 52.6 us  [local(): pl.pallas_call(functools.partial(scorer, sizes), out_shape=jax.ShapeDtype...]
    all_gather x2 -> x0, waiting for transfers between devices: 43.4 us -> none  [the longest x1 43.4 us: local(): lax.all_gather(w_in, 'routers', axis=1, tiled=True)]
    all_to_all x3 -> x0, waiting for transfers between devices: 30.4 us -> none  [the longest x1 13.7 us: local(): lax.all_to_all(attended_slots.reshape(sources, per_source, block_width, h...]
    psum x1 -> x0, waiting for transfers between devices: 16.7 us -> none  [local(): mixed = lax.psum(partial_out, 'heads')]
    all_to_all x3 -> x0, starting transfers between devices: 14.5 us -> none  [the longest x1 6.35 us: local(): lax.all_to_all(slot_user, 'users', split_axis=0, concat_axis=0, tiled=True)]
    dot_general x6 -> x0, matrix products: 13.5 us -> none  [the longest x2 4.92 us: prefix_attention(): jnp.einsum('ghqk,gkhd->gqhd', weights, value_heads, preferred_element_typ...]
    gather x10 -> x0, local copies, waits for them, and re-layouts: 6.47 us -> none  [the longest x1 1.68 us: local(): attended_slots = jnp.take(packed_out, inverse, axis=0)]
    unnamed x32 -> x2, local copies, waits for them, and re-layouts: 7.95 us -> 2.54 us
  transfers between devices with their start and end apart: 6 -> 0, of which waited for: 5 -> 0; matrix products, arithmetic and copies ran while one was open for 18% -> 0% of each run, Pallas kernels for 0% -> 0%
where the time goes in v1:
time: 59.2 us; the launch traced here: 58.9 us
  Pallas kernels  52.6 us (89%)
  local copies, waits for them, and re-layouts  6.32 us (11%)
    pallas_call x1, Pallas kernels, local(): pl.pallas_call(functools.partial(scorer, sizes), out_shape=jax.ShapeDtype...  52.6 us
    unnamed x2, local copies, waits for them, and re-layouts  2.54 us
    reshape x1, local copies, waits for them, and re-layouts, local(): mlp_gain.reshape(1, -1)  1.28 us
    reshape x1, local copies, waits for them, and re-layouts, local(): attn_gain.reshape(1, -1)  1.27 us
    reshape x1, local copies, waits for them, and re-layouts, local(): w_two.reshape(1, -1)  1.23 us

profile of v1, /device:TPU:0, one launch (start us, length us, event | category | flops | bytes accessed | tf_op | source)
XLA Modules:
  0.0 58.9 jit_solution(5757178959156645910)
XLA Ops:
  0.0 1.2 %reshape.11.w_two_ref = bf16[1,256]{1,0:T(2,128)(2,1)} reshape(bf16[256]{0:T(256)(128)(2,1)} %param.23) | data formatting | bytes 1024 | tf_op jit(solution)/shard_map/reshape | solution.py:585
  1.2 1.3 %copy.13.owner_ref = s32[4,1]{1,0:T(4,128)} copy(s32[4,1]{0,1:T(1,128)} %param.13) | data formatting | bytes 32 | tf_op args[1]
  2.5 1.3 %reshape.9.attn_gain_ref = bf16[1,512]{1,0:T(2,128)(2,1)} reshape(bf16[512]{0:T(512)(128)(2,1)} %param.19) | data formatting | bytes 2048 | tf_op jit(solution)/shard_map/reshape | solution.py:581
  3.8 1.3 %reshape.10.mlp_gain_ref = bf16[1,1024]{1,0:T(2,128)(2,1)} reshape(bf16[1024]{0:T(1024)(128)(2,1)} %param.21) | data formatting | bytes 4096 | tf_op jit(solution)/shard_map/reshape | solution.py:583
  5.1 52.6 %shard_map.118 = f32[4,64]{1,0:T(4,128)} custom-call(bf16[4,64,1024]{2,1,0:T(8,128)(2,1)} %items_ref.1, s32[4,1]{1,0:T(4,128)} %copy.13.owner_ref, s32[4]{0:T(128)} %user_ref.1, s32[4]{0:T(128)} %fill_ref.1, bf16[2,256,512]{2,1,0:T(8,128)(2,1)} %keys_ref.1, bf16[2,256,512]{2,1,0:T(8,128)(2,1)} %values_ref.1, bf16[4,512,512]{2,1,0:T(8,128)(2,1)} %w_in_ref.1, ...), custom_call_target="tpu_custom_call" | custom-call | tf_op jit(solution)/shard_map/pallas_call | solution.py:564
  57.7 1.2 %copy.15 = f32[4,64]{1,0:T(4,128)} copy(f32[4,64]{1,0:T(4,128)} %shard_map.118) | data formatting | bytes 2048

commit v2 on v1

--- a/solution.py
+++ b/solution.py
@@ -10,7 +10,6 @@
 HEAD_DIM = 128
 CAP = 2
 EPSILON = 1e-05
-SUB = 2
 F32 = jnp.float32
 BF16 = jnp.bfloat16
 MESH = pl.DeviceIdType.MESH
@@ -69,6 +68,8 @@
     x_recv,
     y_send,
     y_recv,
+    w_send,
+    w_recv,
     st_sem,
     po_send,
     po_recv,
@@ -127,30 +128,32 @@
     c_one = pltpu.make_async_copy(w_one_ref, w_one_v, local_sem.at[5])
     pl.semaphore_wait(barrier, count)
 
-    pieces = [(p, s) for p in range(5) for s in range(SUB)]
-
-    def in_rows(owner_group, s):
-        share = depth // groups // SUB
-        return pl.ds(pl.multiple_of((owner_group * SUB + s) * share, share), share)
-
-    def out_rows(owner_group, s):
-        share = half_width // groups // SUB
-        return pl.ds(pl.multiple_of((owner_group * SUB + s) * share, share), share)
-
-    def weight_slot(owner_router, owner_group, p, s):
+    pieces = [(p, kind) for p in range(5) for kind in range(2)]
+    parity = lax.rem(me, 2)
+    pair = me + 1 - 2 * parity
+
+    def piece_rows(length, kind, owner_group, owner_parity):
+        if kind == 0:
+            share = length // 4 // groups
+            return pl.ds(pl.multiple_of((owner_group * 2 + owner_parity) * share, share), share)
+        share = length // 2 // groups
+        return pl.ds(pl.multiple_of(length // 2 + owner_group * share, share), share)
+
+    def weight_slot(owner_router, owner_group, owner_parity, t):
+        p, kind = pieces[t]
         if p < 4:
-            return w_all.at[p, owner_router, in_rows(owner_group, s), :]
-        return wo_all.at[owner_router, out_rows(owner_group, s), :]
+            return w_all.at[p, owner_router, piece_rows(depth, kind, owner_group, owner_parity), :]
+        return wo_all.at[owner_router, piece_rows(half_width, kind, owner_group, owner_parity), :]
 
     def x_copy(j, t, source_router):
-        p, s = pieces[t]
+        p, kind = pieces[t]
         if p < 4:
-            src = w_in_ref.at[p, in_rows(g, s), :]
+            src = w_in_ref.at[p, piece_rows(depth, kind, g, parity), :]
         else:
-            src = w_o_ref.at[out_rows(g, s), :]
+            src = w_o_ref.at[piece_rows(half_width, kind, g, parity), :]
         return pltpu.make_async_remote_copy(
             src_ref=src,
-            dst_ref=weight_slot(source_router, g, p, s),
+            dst_ref=weight_slot(source_router, g, parity, t),
             send_sem=x_send.at[j, t],
             recv_sem=x_recv.at[j, t],
             device_id={"routers": lax.rem(r + j, routers)},
@@ -158,8 +161,7 @@
         )
 
     def y_copy(i, j, t, owner_group):
-        p, s = pieces[t]
-        spot = weight_slot(lax.rem(r - j + routers, routers), owner_group, p, s)
+        spot = weight_slot(lax.rem(r - j + routers, routers), owner_group, parity, t)
         return pltpu.make_async_remote_copy(
             src_ref=spot,
             dst_ref=spot,
@@ -169,13 +171,26 @@
             device_id_type=MESH,
         )
 
+    def pair_copy(i, j, p, owner_parity):
+        spot = weight_slot(
+            lax.rem(r - j + routers, routers), lax.rem(g - i + groups, groups), owner_parity, 2 * p
+        )
+        return pltpu.make_async_remote_copy(
+            src_ref=spot,
+            dst_ref=spot,
+            send_sem=w_send.at[i, j, p],
+            recv_sem=w_recv.at[i, j, p],
+            device_id={"users": pair},
+            device_id_type=MESH,
+        )
+
     for t in range(len(pieces)):
         for j in range(1, routers):
             x_copy(j, t, r).start()
     for c in (c_win, c_keys, c_values, c_wo, c_one):
         c.start()
 
-    owners = [owner_ref[b, 0] for b in range(blocks)]
+    owners = [owner_ref[b] for b in range(blocks)]
     ranks = []
     for b in range(blocks):
         rank = jnp.int32(0)
@@ -242,27 +257,44 @@
             z_copy(k, me).start()
             m_copy(k, me).start()
 
-    def forward(t):
+    def forward(p, kind):
+        t = 2 * p + kind
         for j in range(1, routers):
             x_copy(j, t, lax.rem(r - j + routers, routers)).wait_recv()
             for i in range(1, groups):
                 y_copy(i, j, t, g).start()
-
-    def landed(t):
+            if kind == 0:
+                pair_copy(0, j, p, parity).start()
+
+    def y_landed(t):
         for j in range(1, routers):
             for i in range(1, groups):
                 y_copy(i, j, t, lax.rem(g - i + groups, groups)).wait_recv()
-
-    forward(0)
-    forward(1)
-    for k in range(1, users):
-        z_copy(k, lax.rem(me - k + users, users)).wait_recv()
-        relay_copy(k, h).start()
-    forward(2)
-    for k in range(1, users):
-        m_copy(k, lax.rem(me - k + users, users)).wait_recv()
-        relay_copy(k, mate).wait_recv()
-    c_win.wait()
+                if t % 2 == 0:
+                    pair_copy(i, j, t // 2, parity).start()
+
+    def landed(p):
+        y_landed(2 * p + 1)
+        for j in range(1, routers):
+            for i in range(groups):
+                pair_copy(i, j, p, 1 - parity).wait_recv()
+
+    def items_landed():
+        for k in range(1, users):
+            z_copy(k, lax.rem(me - k + users, users)).wait_recv()
+            relay_copy(k, h).start()
+        for k in range(1, users):
+            m_copy(k, lax.rem(me - k + users, users)).wait_recv()
+            relay_copy(k, mate).wait_recv()
+
+    for p in range(3):
+        with jax.named_scope(f"fwd{p}"):
+            forward(p, 0)
+            forward(p, 1)
+            y_landed(2 * p)
+    with jax.named_scope("items"):
+        items_landed()
+        c_win.wait()
 
     tile = 4 * width
     tile_slots = 4
@@ -284,15 +316,16 @@
                 )
             target[pl.ds(pl.multiple_of(i * tile, tile), tile), :] = silu(total).astype(target.dtype)
 
-    landed(0)
-    landed(1)
-    project(0, q_v)
-    forward(3)
+    with jax.named_scope("land0"):
+        landed(0)
+    with jax.named_scope("proj0"):
+        project(0, q_v)
+    with jax.named_scope("fwd3a"):
+        forward(3, 0)
     c_keys.wait()
     c_values.wait()
 
-    @pl.loop(0, tiles)
-    def _(i):
+    def attend(i):
         span = pl.ds(pl.multiple_of(i * tile, tile), tile)
         for e in range(heads_here):
             cols = slice(e * HEAD_DIM, (e + 1) * HEAD_DIM)
@@ -318,16 +351,23 @@
                 .astype(F32)
             )
 
-    forward(4)
-    landed(2)
-    landed(3)
-    project(1, sk_v)
-    forward(5)
-    forward(6)
-    landed(4)
-    landed(5)
-    project(2, sv_v)
-    forward(7)
+    with jax.named_scope("attend0"):
+        pl.loop(0, tiles // 2)(attend)
+    with jax.named_scope("fwd3b"):
+        forward(3, 1)
+        y_landed(6)
+    with jax.named_scope("attend1"):
+        pl.loop(tiles // 2, tiles)(attend)
+    with jax.named_scope("land1"):
+        landed(1)
+    with jax.named_scope("proj1"):
+        project(1, sk_v)
+    with jax.named_scope("fwd4a"):
+        forward(4, 0)
+    with jax.named_scope("land2"):
+        landed(2)
+    with jax.named_scope("proj2"):
+        project(2, sv_v)
 
     lane = lax.broadcasted_iota(jnp.int32, (tile, 128), 1)
 
@@ -354,12 +394,15 @@
         device_id_type=MESH,
     )
     stat_copy.start()
-    forward(8)
-    landed(6)
-    landed(7)
-    project(3, gates_v)
-    forward(9)
-    stat_copy.wait_recv()
+    with jax.named_scope("fwd4b"):
+        forward(4, 1)
+        y_landed(8)
+    with jax.named_scope("land3"):
+        landed(3)
+    with jax.named_scope("proj3"):
+        project(3, gates_v)
+    with jax.named_scope("statwait"):
+        stat_copy.wait_recv()
 
     @pl.loop(0, tiles)
     def _(i):
@@ -370,7 +413,7 @@
         gated_v[span, :] = (
             (att_v[span, :] - mean)
             * lax.rsqrt(var + EPSILON)
-            * attn_gain_ref[...].astype(F32)
+            * attn_gain_ref[...].astype(F32).reshape(1, -1)
             * gates_v[span, :]
         ).astype(BF16)
 
@@ -401,19 +444,20 @@
     out_project(0, mate, part_out)
     part_copy(0).start()
     out_project(0, h, part_own)
-    landed(8)
-    landed(9)
+    with jax.named_scope("land4"):
+        landed(4)
     for j in range(1, routers):
         out_project(j, mate, part_out)
         part_copy(j).start()
     for j in range(1, routers):
         out_project(j, h, part_own)
     c_one.wait()
-    for j in range(routers):
-        part_copy(j).wait_recv()
+    with jax.named_scope("partwait"):
+        for j in range(routers):
+            part_copy(j).wait_recv()
 
     sources_tile = tile_slots // CAP
-    two = jnp.broadcast_to(w_two_ref[...], (8, w_two_ref.shape[1]))
+    two = jnp.broadcast_to(w_two_ref[...].astype(F32).reshape(1, -1), (8, w_two_ref.shape[0])).astype(BF16)
 
     @pl.loop(0, half_tiles)
     def _(i):
@@ -425,7 +469,7 @@
             mixed.append(part_own[j, span, :] + part_in[j, span, :])
         residual = x + jnp.concatenate(mixed, axis=1)
         norm = lax.rsqrt(jnp.sum(residual * residual, axis=1, keepdims=True) / model + EPSILON)
-        normed = (residual * norm * mlp_gain_ref[...].astype(F32)).astype(BF16)
+        normed = (residual * norm * mlp_gain_ref[...].astype(F32).reshape(1, -1)).astype(BF16)
         hidden = silu(jnp.dot(normed, w_one_v[...], preferred_element_type=F32)).astype(BF16)
         found = lax.dot_general(two, hidden, (((1,), (1,)), ((), ())), preferred_element_type=F32)
         for s in range(sources_tile):
@@ -457,11 +501,12 @@
                 ret[me] = sc_out[i]
 
     handler = me // mine
-    for d in range(users):
-
-        @pl.when(jnp.logical_not((d == me) & (h == handler)))
-        def _():
-            score_copy(0, 0, d, d).wait_recv()
+    with jax.named_scope("scorewait"):
+        for d in range(users):
+
+            @pl.when(jnp.logical_not((d == me) & (h == handler)))
+            def _():
+                score_copy(0, 0, d, d).wait_recv()
 
     position = lax.broadcasted_iota(jnp.int32, (1, width), 1)
     for b in range(blocks):
@@ -476,6 +521,10 @@
             x_copy(j, t, r).wait_send()
             for i in range(1, groups):
                 y_copy(i, j, t, g).wait_send()
+    for p in range(5):
+        for j in range(1, routers):
+            for i in range(groups):
+                pair_copy(i, j, p, parity).wait_send()
     for k in range(1, users):
         z_copy(k, me).wait_send()
         m_copy(k, me).wait_send()
@@ -515,7 +564,7 @@
     out_cols = w_o.shape[1]
     cached, per_user, _ = prefix_keys.shape
     positions = cached * per_user
-    pieces = 5 * SUB
+    pieces = 10
     dma = pltpu.SemaphoreType.DMA
     hbm = pl.BlockSpec(memory_space=pl.ANY)
     vmem = pl.BlockSpec(memory_space=pltpu.VMEM)
@@ -555,6 +604,8 @@
         dma((routers, pieces)),
         dma((groups, routers, pieces)),
         dma((groups, routers, pieces)),
+        dma((groups, routers, 5)),
+        dma((groups, routers, 5)),
         dma((2,)),
         dma((routers,)),
         dma((routers,)),
@@ -572,17 +623,17 @@
         ),
     )(
         items,
-        block_owner,
+        block_owner.reshape(-1),
         block_user,
         block_fill,
         prefix_keys,
         prefix_values,
         w_in,
-        attn_gain.reshape(1, -1),
+        attn_gain,
         w_o,
-        mlp_gain.reshape(1, -1),
+        mlp_gain,
         w_one,
-        w_two.reshape(1, -1),
+        w_two,
     )
 
 

time: 59.2 us -> 46.3 us (0.78)
  Pallas kernels: 52.6 us -> 44.8 us
  local copies, waits for them, and re-layouts: 6.32 us -> 1.26 us
    pallas_call x1, Pallas kernels: 52.6 us -> 44.8 us  [local(): pl.pallas_call(functools.partial(scorer, sizes), out_shape=jax.ShapeDtype...]
    reshape x3 -> x0, local copies, waits for them, and re-layouts: 3.78 us -> none  [the longest x1 1.28 us: local(): mlp_gain.reshape(1, -1)]
    unnamed x2 -> x1, local copies, waits for them, and re-layouts: 2.54 us -> 1.26 us
where the time goes in v2:
time: 46.3 us; the launch traced here: 46.1 us
  Pallas kernels  44.8 us (97%)
  local copies, waits for them, and re-layouts  1.26 us (3%)
    pallas_call x1, Pallas kernels, local(): pl.pallas_call(functools.partial(scorer, sizes), out_shape=jax.ShapeDtype...  44.8 us
    unnamed x1, local copies, waits for them, and re-layouts  1.26 us

profile of v2, /device:TPU:0, one launch (start us, length us, event | category | flops | bytes accessed | tf_op | source)
XLA Modules:
  0.0 46.1 jit_solution(3993267940068705207)
XLA Ops:
  0.0 44.8 %shard_map.118 = f32[4,64]{1,0:T(4,128)} custom-call(bf16[4,64,1024]{2,1,0:T(8,128)(2,1)} %items_ref.1, s32[4]{0:T(128)} %bitcast.1, s32[4]{0:T(128)} %user_ref.1, s32[4]{0:T(128)} %fill_ref.1, bf16[2,256,512]{2,1,0:T(8,128)(2,1)} %keys_ref.1, bf16[2,256,512]{2,1,0:T(8,128)(2,1)} %values_ref.1, bf16[4,512,512]{2,1,0:T(8,128)(2,1)} %w_in_ref.1, ...), custom_call_target="tpu_custom_call" | custom-call | tf_op jit(solution)/shard_map/pallas_call | solution.py:615
  44.9 1.3 %copy.14 = f32[4,64]{1,0:T(4,128)} copy(f32[4,64]{1,0:T(4,128)} %shard_map.118) | data formatting | bytes 2048

commit v3 on v2

--- a/solution.py
+++ b/solution.py
@@ -1,4 +1,5 @@
 import functools
+import math
 
 import jax
 import jax.numpy as jnp
@@ -10,6 +11,13 @@
 HEAD_DIM = 128
 CAP = 2
 EPSILON = 1e-05
+TREE_EIGHTHS = (0, 5, 5, 5, 4)
+PARTS = (4, 1, 1, 1, 4)
+ORDER = (
+    [(0, "g", part) for part in range(PARTS[0])]
+    + [(1, "t", 0), (2, "t", 0), (1, "g", 0), (3, "t", 0), (4, "t", 0), (2, "g", 0), (3, "g", 0)]
+    + [(4, "g", part) for part in range(PARTS[4])]
+)
 F32 = jnp.float32
 BF16 = jnp.bfloat16
 MESH = pl.DeviceIdType.MESH
@@ -45,9 +53,7 @@
     wo_all,
     w_one_v,
     q_v,
-    sk_v,
-    sv_v,
-    gates_v,
+    own_v,
     att_v,
     gated_v,
     stat_out,
@@ -128,29 +134,32 @@
     c_one = pltpu.make_async_copy(w_one_ref, w_one_v, local_sem.at[5])
     pl.semaphore_wait(barrier, count)
 
-    pieces = [(p, kind) for p in range(5) for kind in range(2)]
+    pieces = ORDER
+    number = {piece: t for t, piece in enumerate(pieces)}
     parity = lax.rem(me, 2)
     pair = me + 1 - 2 * parity
 
-    def piece_rows(length, kind, owner_group, owner_parity):
-        if kind == 0:
-            share = length // 4 // groups
-            return pl.ds(pl.multiple_of((owner_group * 2 + owner_parity) * share, share), share)
-        share = length // 2 // groups
-        return pl.ds(pl.multiple_of(length // 2 + owner_group * share, share), share)
+    def piece_rows(p, kind, part, owner_group, owner_parity):
+        length = depth if p < 4 else half_width
+        tree = length * TREE_EIGHTHS[p] // 8 // (2 * groups) // 16 * 16
+        if kind == "t":
+            return pl.ds(pl.multiple_of((owner_group * 2 + owner_parity) * tree, tree), tree)
+        direct = length // groups - 2 * tree
+        share = direct // PARTS[p]
+        start = 2 * groups * tree + owner_group * direct + part * share
+        return pl.ds(pl.multiple_of(start, math.gcd(share, 16)), share)
 
     def weight_slot(owner_router, owner_group, owner_parity, t):
-        p, kind = pieces[t]
+        p, kind, part = pieces[t]
+        span = piece_rows(p, kind, part, owner_group, owner_parity)
         if p < 4:
-            return w_all.at[p, owner_router, piece_rows(depth, kind, owner_group, owner_parity), :]
-        return wo_all.at[owner_router, piece_rows(half_width, kind, owner_group, owner_parity), :]
+            return w_all.at[p, owner_router, span, :]
+        return wo_all.at[owner_router, span, :]
 
     def x_copy(j, t, source_router):
-        p, kind = pieces[t]
-        if p < 4:
-            src = w_in_ref.at[p, piece_rows(depth, kind, g, parity), :]
-        else:
-            src = w_o_ref.at[piece_rows(half_width, kind, g, parity), :]
+        p, kind, part = pieces[t]
+        span = piece_rows(p, kind, part, g, parity)
+        src = w_in_ref.at[p, span, :] if p < 4 else w_o_ref.at[span, :]
         return pltpu.make_async_remote_copy(
             src_ref=src,
             dst_ref=weight_slot(source_router, g, parity, t),
@@ -173,7 +182,10 @@
 
     def pair_copy(i, j, p, owner_parity):
         spot = weight_slot(
-            lax.rem(r - j + routers, routers), lax.rem(g - i + groups, groups), owner_parity, 2 * p
+            lax.rem(r - j + routers, routers),
+            lax.rem(g - i + groups, groups),
+            owner_parity,
+            number[p, "t", 0],
         )
         return pltpu.make_async_remote_copy(
             src_ref=spot,
@@ -257,76 +269,55 @@
             z_copy(k, me).start()
             m_copy(k, me).start()
 
-    def forward(p, kind):
-        t = 2 * p + kind
+    def forward(p, kind, part=0):
+        t = number[p, kind, part]
         for j in range(1, routers):
             x_copy(j, t, lax.rem(r - j + routers, routers)).wait_recv()
             for i in range(1, groups):
                 y_copy(i, j, t, g).start()
-            if kind == 0:
+            if kind == "t":
                 pair_copy(0, j, p, parity).start()
 
-    def y_landed(t):
+    def y_landed(p, kind, part=0):
+        t = number[p, kind, part]
         for j in range(1, routers):
             for i in range(1, groups):
                 y_copy(i, j, t, lax.rem(g - i + groups, groups)).wait_recv()
-                if t % 2 == 0:
-                    pair_copy(i, j, t // 2, parity).start()
+                if kind == "t":
+                    pair_copy(i, j, p, parity).start()
 
     def landed(p):
-        y_landed(2 * p + 1)
-        for j in range(1, routers):
-            for i in range(groups):
-                pair_copy(i, j, p, 1 - parity).wait_recv()
-
-    def items_landed():
-        for k in range(1, users):
-            z_copy(k, lax.rem(me - k + users, users)).wait_recv()
-            relay_copy(k, h).start()
-        for k in range(1, users):
-            m_copy(k, lax.rem(me - k + users, users)).wait_recv()
-            relay_copy(k, mate).wait_recv()
-
-    for p in range(3):
-        with jax.named_scope(f"fwd{p}"):
-            forward(p, 0)
-            forward(p, 1)
-            y_landed(2 * p)
-    with jax.named_scope("items"):
-        items_landed()
-        c_win.wait()
-
-    tile = 4 * width
+        for part in range(PARTS[p]):
+            y_landed(p, "g", part)
+        if TREE_EIGHTHS[p]:
+            for j in range(1, routers):
+                for i in range(groups):
+                    pair_copy(i, j, p, 1 - parity).wait_recv()
+
     tile_slots = 4
+    tile = tile_slots * width
     tiles = rows // tile
 
     def x_tile(i):
         return x_all[pl.ds(i * tile_slots, tile_slots)].reshape(tile, model)
 
-    def project(p, target):
-        @pl.loop(0, tiles)
-        def _(i):
-            x = x_tile(i)
-            total = jnp.zeros((tile, half_width), F32)
-            for a in range(routers):
-                total = total + jnp.dot(
-                    x[:, a * depth : (a + 1) * depth],
-                    w_all[p, a],
-                    preferred_element_type=F32,
-                )
-            target[pl.ds(pl.multiple_of(i * tile, tile), tile), :] = silu(total).astype(target.dtype)
-
-    with jax.named_scope("land0"):
-        landed(0)
-    with jax.named_scope("proj0"):
-        project(0, q_v)
-    with jax.named_scope("fwd3a"):
-        forward(3, 0)
-    c_keys.wait()
-    c_values.wait()
+    def span_of(i):
+        return pl.ds(pl.multiple_of(i * tile, tile), tile)
+
+    def projected(p, i):
+        x = x_tile(i)
+        total = jnp.zeros((tile, half_width), F32)
+        for a in range(routers):
+            total = total + jnp.dot(
+                x[:, a * depth : (a + 1) * depth], w_all[p, a], preferred_element_type=F32
+            )
+        return silu(total)
+
+    def query(i):
+        q_v[span_of(i), :] = projected(0, i).astype(BF16)
 
     def attend(i):
-        span = pl.ds(pl.multiple_of(i * tile, tile), tile)
+        span = span_of(i)
         for e in range(heads_here):
             cols = slice(e * HEAD_DIM, (e + 1) * HEAD_DIM)
             raw = lax.dot_general(
@@ -351,39 +342,89 @@
                 .astype(F32)
             )
 
+    def self_key(i):
+        span = span_of(i)
+        keys = projected(1, i)
+        for e in range(heads_here):
+            cols = slice(e * HEAD_DIM, (e + 1) * HEAD_DIM)
+            own = jnp.sum(q_v[span, cols].astype(F32) * keys[:, cols], axis=1, keepdims=True)
+            own_v[span, cols] = jnp.broadcast_to(silu(own * scale), (tile, HEAD_DIM))
+
+    lane = lax.broadcasted_iota(jnp.int32, (tile, 128), 1)
+
+    def self_value(i):
+        span = span_of(i)
+        att = att_v[span, :] + own_v[span, :] * projected(2, i)
+        att_v[span, :] = att
+        total = jnp.sum(att, axis=1, keepdims=True)
+        square = jnp.sum(att * att, axis=1, keepdims=True)
+        stat_out[span, :] = jnp.where(lane == 0, total, square)
+
+    def gate(i):
+        span = span_of(i)
+        both = stat_out[span, :] + stat_in[span, :]
+        mean = both[:, 0:1] / hd_all
+        var = both[:, 1:2] / hd_all - mean * mean
+        gated_v[span, :] = (
+            (att_v[span, :] - mean)
+            * lax.rsqrt(var + EPSILON)
+            * attn_gain_ref[...].astype(F32).reshape(1, -1)
+            * projected(3, i)
+        ).astype(BF16)
+
+    with jax.named_scope("fwd0"):
+        for part in range(PARTS[0]):
+            forward(0, "g", part)
+    with jax.named_scope("fwd1"):
+        forward(1, "t")
+        forward(2, "t")
+    with jax.named_scope("items"):
+        for k in range(1, users):
+            z_copy(k, lax.rem(me - k + users, users)).wait_recv()
+            relay_copy(k, h).start()
+    with jax.named_scope("fwd1b"):
+        forward(1, "g")
+        y_landed(1, "t")
+    with jax.named_scope("items2"):
+        for k in range(1, users):
+            m_copy(k, lax.rem(me - k + users, users)).wait_recv()
+            relay_copy(k, mate).wait_recv()
+        c_win.wait()
+    with jax.named_scope("land0"):
+        landed(0)
+    with jax.named_scope("query"):
+        pl.loop(0, tiles)(query)
+    with jax.named_scope("fwd3a"):
+        forward(3, "t")
+        y_landed(2, "t")
+    c_keys.wait()
+    c_values.wait()
     with jax.named_scope("attend0"):
         pl.loop(0, tiles // 2)(attend)
-    with jax.named_scope("fwd3b"):
-        forward(3, 1)
-        y_landed(6)
+    with jax.named_scope("fwd4a"):
+        forward(4, "t")
     with jax.named_scope("attend1"):
         pl.loop(tiles // 2, tiles)(attend)
+    with jax.named_scope("fwd2b"):
+        forward(2, "g")
     with jax.named_scope("land1"):
         landed(1)
-    with jax.named_scope("proj1"):
-        project(1, sk_v)
-    with jax.named_scope("fwd4a"):
-        forward(4, 0)
+    with jax.named_scope("key"):
+        pl.loop(0, tiles)(self_key)
+    with jax.named_scope("fwd3b"):
+        forward(3, "g")
+        y_landed(3, "t")
+        forward(4, "g", 0)
+        y_landed(4, "t")
+        forward(4, "g", 1)
     with jax.named_scope("land2"):
         landed(2)
-    with jax.named_scope("proj2"):
-        project(2, sv_v)
-
-    lane = lax.broadcasted_iota(jnp.int32, (tile, 128), 1)
-
-    @pl.loop(0, tiles)
-    def _(i):
-        span = pl.ds(pl.multiple_of(i * tile, tile), tile)
-        total = jnp.zeros((tile, 1), F32)
-        square = jnp.zeros((tile, 1), F32)
-        for e in range(heads_here):
-            cols = slice(e * HEAD_DIM, (e + 1) * HEAD_DIM)
-            own = jnp.sum(q_v[span, cols].astype(F32) * sk_v[span, cols], axis=1, keepdims=True)
-            att = att_v[span, cols] + silu(own * scale) * sv_v[span, cols]
-            att_v[span, cols] = att
-            total = total + jnp.sum(att, axis=1, keepdims=True)
-            square = square + jnp.sum(att * att, axis=1, keepdims=True)
-        stat_out[span, :] = jnp.where(lane == 0, total, square)
+    with jax.named_scope("value0"):
+        pl.loop(0, tiles // 2)(self_value)
+    with jax.named_scope("fwd4c"):
+        forward(4, "g", 2)
+    with jax.named_scope("value1"):
+        pl.loop(tiles // 2, tiles)(self_value)
 
     stat_copy = pltpu.make_async_remote_copy(
         src_ref=stat_out,
@@ -395,87 +436,80 @@
     )
     stat_copy.start()
     with jax.named_scope("fwd4b"):
-        forward(4, 1)
-        y_landed(8)
+        forward(4, "g", 3)
     with jax.named_scope("land3"):
         landed(3)
-    with jax.named_scope("proj3"):
-        project(3, gates_v)
     with jax.named_scope("statwait"):
         stat_copy.wait_recv()
-
-    @pl.loop(0, tiles)
-    def _(i):
-        span = pl.ds(pl.multiple_of(i * tile, tile), tile)
-        both = stat_out[span, :] + stat_in[span, :]
-        mean = both[:, 0:1] / hd_all
-        var = both[:, 1:2] / hd_all - mean * mean
-        gated_v[span, :] = (
-            (att_v[span, :] - mean)
-            * lax.rsqrt(var + EPSILON)
-            * attn_gain_ref[...].astype(F32).reshape(1, -1)
-            * gates_v[span, :]
-        ).astype(BF16)
+    with jax.named_scope("gate"):
+        pl.loop(0, tiles)(gate)
 
     half = rows // heads
-    half_tiles = half // tile
     c_wo.wait()
 
-    def part_copy(j):
+    mine = users // heads
+    piece = half // 2
+    source_rows = CAP * width
+
+    def far_first(e, i, amount):
+        return jnp.where(me < e * mine + mine // 2, amount - 1 - i, i)
+
+    def part_copy(j, c):
+        spot = pl.ds(pl.multiple_of(c * piece, piece), piece)
         return pltpu.make_async_remote_copy(
-            src_ref=part_out.at[j],
-            dst_ref=part_in.at[j],
-            send_sem=po_send.at[j],
-            recv_sem=po_recv.at[j],
+            src_ref=part_out.at[j, spot, :],
+            dst_ref=part_in.at[j, spot, :],
+            send_sem=po_send.at[j, c],
+            recv_sem=po_recv.at[j, c],
             device_id={"heads": mate},
             device_id_type=MESH,
         )
 
-    def out_project(j, row_half, target):
-        a = lax.rem(r - j + routers, routers)
-
-        @pl.loop(0, half_tiles)
-        def _(i):
-            src = pl.ds(pl.multiple_of(row_half * half + i * tile, tile), tile)
-            target[j, pl.ds(pl.multiple_of(i * tile, tile), tile), :] = jnp.dot(
-                gated_v[src, :], wo_all[a], preferred_element_type=F32
-            )
-
-    out_project(0, mate, part_out)
-    part_copy(0).start()
-    out_project(0, h, part_own)
+    def out_project(j, row_half, c, target):
+        src = pl.ds(pl.multiple_of(row_half * half + c * piece, piece), piece)
+        target[j, pl.ds(pl.multiple_of(c * piece, piece), piece), :] = jnp.dot(
+            gated_v[src, :],
+            wo_all[lax.rem(r - j + routers, routers)],
+            preferred_element_type=F32,
+        ).astype(target.dtype)
+
+    def shares(j):
+        for i in range(2):
+            c = far_first(mate, i, 2)
+            out_project(j, mate, c, part_out)
+            part_copy(j, c).start()
+
+    with jax.named_scope("outown"):
+        shares(0)
+        for c in range(2):
+            out_project(0, h, c, part_own)
     with jax.named_scope("land4"):
         landed(4)
     for j in range(1, routers):
-        out_project(j, mate, part_out)
-        part_copy(j).start()
+        shares(j)
     for j in range(1, routers):
-        out_project(j, h, part_own)
+        for c in range(2):
+            out_project(j, h, c, part_own)
     c_one.wait()
-    with jax.named_scope("partwait"):
-        for j in range(routers):
-            part_copy(j).wait_recv()
-
-    sources_tile = tile_slots // CAP
-    two = jnp.broadcast_to(w_two_ref[...].astype(F32).reshape(1, -1), (8, w_two_ref.shape[0])).astype(BF16)
-
-    @pl.loop(0, half_tiles)
-    def _(i):
-        span = pl.ds(pl.multiple_of(i * tile, tile), tile)
-        x = x_tile(h * half_tiles + i).astype(F32)
+
+    two = jnp.broadcast_to(
+        w_two_ref[...].astype(F32).reshape(1, -1), (8, w_two_ref.shape[0])
+    ).astype(BF16)
+
+    def score(source, i):
+        span = pl.ds(pl.multiple_of(source * source_rows, source_rows), source_rows)
+        x = x_all[pl.ds((h * mine + source) * CAP, CAP)].reshape(source_rows, model).astype(F32)
         mixed = []
         for a in range(routers):
             j = lax.rem(r - a + routers, routers)
-            mixed.append(part_own[j, span, :] + part_in[j, span, :])
+            mixed.append(part_own[j, span, :] + part_in[j, span, :].astype(F32))
         residual = x + jnp.concatenate(mixed, axis=1)
         norm = lax.rsqrt(jnp.sum(residual * residual, axis=1, keepdims=True) / model + EPSILON)
         normed = (residual * norm * mlp_gain_ref[...].astype(F32).reshape(1, -1)).astype(BF16)
         hidden = silu(jnp.dot(normed, w_one_v[...], preferred_element_type=F32)).astype(BF16)
-        found = lax.dot_general(two, hidden, (((1,), (1,)), ((), ())), preferred_element_type=F32)
-        for s in range(sources_tile):
-            sc_out[i * sources_tile + s] = found[:, s * CAP * width : (s + 1) * CAP * width]
-
-    mine = users // heads
+        sc_out[i] = lax.dot_general(
+            two, hidden, (((1,), (1,)), ((), ())), preferred_element_type=F32
+        )
 
     def score_copy(i, e, owner, sem):
         return pltpu.make_async_remote_copy(
@@ -483,12 +517,18 @@
             dst_ref=ret.at[owner],
             send_sem=sc_send.at[i, e],
             recv_sem=sc_recv.at[sem],
-            device_id={"users": h * mine + i, "heads": e},
+            device_id={"users": h * mine + far_first(h, i, mine), "heads": e},
             device_id_type=MESH,
         )
 
     for i in range(mine):
-        target = h * mine + i
+        source = far_first(h, i, mine)
+        if i % (mine // 2) == 0:
+            with jax.named_scope("partwait"):
+                for j in range(routers):
+                    part_copy(j, far_first(h, i // (mine // 2), 2)).wait_recv()
+        score(source, i)
+        target = h * mine + source
         for e in range(heads):
             itself = (target == me) & (h == e)
 
@@ -522,20 +562,22 @@
             for i in range(1, groups):
                 y_copy(i, j, t, g).wait_send()
     for p in range(5):
-        for j in range(1, routers):
-            for i in range(groups):
-                pair_copy(i, j, p, parity).wait_send()
+        if TREE_EIGHTHS[p]:
+            for j in range(1, routers):
+                for i in range(groups):
+                    pair_copy(i, j, p, parity).wait_send()
     for k in range(1, users):
         z_copy(k, me).wait_send()
         m_copy(k, me).wait_send()
         relay_copy(k, h).wait_send()
     stat_copy.wait_send()
     for j in range(routers):
-        part_copy(j).wait_send()
+        for c in range(2):
+            part_copy(j, c).wait_send()
     for i in range(mine):
         for e in range(heads):
 
-            @pl.when(jnp.logical_not((h * mine + i == me) & (h == e)))
+            @pl.when(jnp.logical_not((h * mine + far_first(h, i, mine) == me) & (h == e)))
             def _():
                 score_copy(i, e, me, me).wait_send()
 
@@ -564,7 +606,7 @@
     out_cols = w_o.shape[1]
     cached, per_user, _ = prefix_keys.shape
     positions = cached * per_user
-    pieces = 10
+    pieces = len(ORDER)
     dma = pltpu.SemaphoreType.DMA
     hbm = pl.BlockSpec(memory_space=pl.ANY)
     vmem = pl.BlockSpec(memory_space=pltpu.VMEM)
@@ -583,14 +625,12 @@
         pltpu.VMEM((rows, half_width), BF16),
         pltpu.VMEM((rows, half_width), F32),
         pltpu.VMEM((rows, half_width), F32),
-        pltpu.VMEM((rows, half_width), F32),
-        pltpu.VMEM((rows, half_width), F32),
         pltpu.VMEM((rows, half_width), BF16),
         pltpu.VMEM((rows, 128), F32),
         pltpu.VMEM((rows, 128), F32),
+        pltpu.VMEM((routers, half, out_cols), BF16),
         pltpu.VMEM((routers, half, out_cols), F32),
-        pltpu.VMEM((routers, half, out_cols), F32),
-        pltpu.VMEM((routers, half, out_cols), F32),
+        pltpu.VMEM((routers, half, out_cols), BF16),
         pltpu.VMEM((users // heads, 8, CAP * width), F32),
         pltpu.VMEM((users, 8, CAP * width), F32),
         dma((6,)),
@@ -607,8 +647,8 @@
         dma((groups, routers, 5)),
         dma((groups, routers, 5)),
         dma((2,)),
-        dma((routers,)),
-        dma((routers,)),
+        dma((routers, 2)),
+        dma((routers, 2)),
         dma((users // heads, heads)),
         dma((users,)),
     ]

time: 46.3 us -> 44.8 us (0.968)
  Pallas kernels: 44.8 us -> 43.4 us
    pallas_call x1, Pallas kernels: 44.8 us -> 43.4 us  [local(): pl.pallas_call(functools.partial(scorer, sizes), out_shape=jax.ShapeDtype...]
where the time goes in v3:
time: 44.8 us; the launch traced here: 44.6 us
  Pallas kernels  43.4 us (97%)
  local copies, waits for them, and re-layouts  1.26 us (3%)
    pallas_call x1, Pallas kernels, local(): pl.pallas_call(functools.partial(scorer, sizes), out_shape=jax.ShapeDtype...  43.4 us
    unnamed x1, local copies, waits for them, and re-layouts  1.26 us

profile of v3, /device:TPU:0, one launch (start us, length us, event | category | flops | bytes accessed | tf_op | source)
XLA Modules:
  0.0 44.6 jit_solution(13437704585005342916)
XLA Ops:
  0.0 43.4 %shard_map.118 = f32[4,64]{1,0:T(4,128)} custom-call(bf16[4,64,1024]{2,1,0:T(8,128)(2,1)} %items_ref.1, s32[4]{0:T(128)} %bitcast.1, s32[4]{0:T(128)} %user_ref.1, s32[4]{0:T(128)} %fill_ref.1, bf16[2,256,512]{2,1,0:T(8,128)(2,1)} %keys_ref.1, bf16[2,256,512]{2,1,0:T(8,128)(2,1)} %values_ref.1, bf16[4,512,512]{2,1,0:T(8,128)(2,1)} %w_in_ref.1, ...), custom_call_target="tpu_custom_call" | custom-call | tf_op jit(solution)/shard_map/pallas_call | solution.py:655
  43.4 1.3 %copy.14 = f32[4,64]{1,0:T(4,128)} copy(f32[4,64]{1,0:T(4,128)} %shard_map.118) | data formatting | bytes 2048

commit v4 on v3

--- a/solution.py
+++ b/solution.py
@@ -378,12 +378,12 @@
     with jax.named_scope("fwd1"):
         forward(1, "t")
         forward(2, "t")
+        forward(1, "g")
     with jax.named_scope("items"):
         for k in range(1, users):
             z_copy(k, lax.rem(me - k + users, users)).wait_recv()
             relay_copy(k, h).start()
     with jax.named_scope("fwd1b"):
-        forward(1, "g")
         y_landed(1, "t")
     with jax.named_scope("items2"):
         for k in range(1, users):

time: 44.8 us -> 44.8 us (level)
  no operation moved by 1% of the time
where the time goes in v4:
time: 44.8 us; the launch traced here: 44.6 us
  Pallas kernels  43.4 us (97%)
  local copies, waits for them, and re-layouts  1.26 us (3%)
    pallas_call x1, Pallas kernels, local(): pl.pallas_call(functools.partial(scorer, sizes), out_shape=jax.ShapeDtype...  43.4 us
    unnamed x1, local copies, waits for them, and re-layouts  1.26 us

profile of v4, /device:TPU:0, one launch (start us, length us, event | category | flops | bytes accessed | tf_op | source)
XLA Modules:
  0.0 44.6 jit_solution(1481759475760965565)
XLA Ops:
  0.0 43.4 %shard_map.118 = f32[4,64]{1,0:T(4,128)} custom-call(bf16[4,64,1024]{2,1,0:T(8,128)(2,1)} %items_ref.1, s32[4]{0:T(128)} %bitcast.1, s32[4]{0:T(128)} %user_ref.1, s32[4]{0:T(128)} %fill_ref.1, bf16[2,256,512]{2,1,0:T(8,128)(2,1)} %keys_ref.1, bf16[2,256,512]{2,1,0:T(8,128)(2,1)} %values_ref.1, bf16[4,512,512]{2,1,0:T(8,128)(2,1)} %w_in_ref.1, ...), custom_call_target="tpu_custom_call" | custom-call | tf_op jit(solution)/shard_map/pallas_call | solution.py:655
  43.4 1.3 %copy.14 = f32[4,64]{1,0:T(4,128)} copy(f32[4,64]{1,0:T(4,128)} %shard_map.118) | data formatting | bytes 2048
